TPU v7x, 32 devices: a whole 2x2x4 slice. The times are simulated.
32 devices in a mesh: dp: 4 (over y, x), row: 4 (over z), col: 2 (over core).
Axes of the slice: x: 2, y: 2, z: 4, core: 2. Of those that a mesh axis runs over, the one named last changes fastest.
Arguments:
- activations: bfloat16 [4, 64, 128, 512], P('dp', None, 'row', 'col'), may hold values from -18 to 18
- kernel: bfloat16 [3, 3, 64, 64], replicated, may hold values from -0.125 to 0.125
- gain: float32 [64], replicated, may hold values from 0.25 to 1.75
- cotangent: bfloat16 [4, 64, 128, 512], P('dp', None, 'row', 'col'), may hold values from -16 to 16
Outputs:
- input_grad: bfloat16 [4, 64, 128, 512], P('dp', None, 'row', 'col')
- weight_grad: float32 [3, 3, 64, 64], P(None, None, 'dp')
- gain_grad: float32 [64], replicated
- shift_grad: float32 [64], replicated
All inputs are finite; a program needn't handle non-finite values.
Results may differ from a plain program's by a relative error of at most 0.0049.
Values may be sent and summed in bfloat16 or wider, within the bound.
A program may use at most 64 MiB of HBM per device.

v0:
```python
import jax
import jax.numpy as jnp
from jax import lax
from jax.sharding import PartitionSpec as P


def with_halo(shard, sides, width):
    for axis, dim in sides:
        count, length = (lax.axis_size(axis), shard.shape[dim])
        up = [(i, (i + 1) % count) for i in range(count - 1)]
        down = [(j, i) for i, j in up]
        last = lax.slice_in_dim(shard, length - width, length, axis=dim)
        initial = lax.slice_in_dim(shard, 0, width, axis=dim)
        before = lax.ppermute(last, axis, up)
        after = lax.ppermute(initial, axis, down)
        shard = jnp.concatenate([before, shard, after], axis=dim)
    return shard


def per_device(activations, kernel, gain, cotangent):
    images, channels, height, width = activations.shape
    total = jnp.float32(
        images * height * width * lax.axis_size("dp") * lax.axis_size("row") * lax.axis_size("col")
    )
    padded = with_halo(activations, (("row", 2), ("col", 3)), 1)
    pre = jnp.zeros((images, channels, height, width), jnp.float32)
    for tap_row in range(3):
        for tap_col in range(3):
            window = padded[:, :, tap_row : tap_row + height, tap_col : tap_col + width]
            pre = pre + jnp.einsum(
                "oc,bchw->bohw",
                kernel[tap_row, tap_col],
                window,
                preferred_element_type=jnp.float32,
            )
    grad = cotangent.astype(jnp.float32)
    local_pre = jnp.sum(pre, axis=(0, 2, 3))
    local_sq = jnp.sum(pre * pre, axis=(0, 2, 3))
    local_cot = jnp.sum(grad, axis=(0, 2, 3))
    local_cross = jnp.sum(grad * pre, axis=(0, 2, 3))
    sum_pre, sum_sq, sum_cot, sum_cross = lax.psum(
        (local_pre, local_sq, local_cot, local_cross), ("dp", "row", "col")
    )
    mean = sum_pre / total
    rstd = lax.rsqrt(sum_sq / total - mean * mean + 1e-05)
    sum_norm = (sum_cross - mean * sum_cot) * rstd
    normed = (pre - mean[:, None, None]) * rstd[:, None, None]
    pre_grad = (gain * rstd)[:, None, None] * (
        grad - (sum_cot / total)[:, None, None] - normed * (sum_norm / total)[:, None, None]
    )
    pre_grad = pre_grad.astype(jnp.bfloat16)
    grad_padded = with_halo(pre_grad, (("row", 2), ("col", 3)), 1)
    input_grad = jnp.zeros((images, channels, height, width), jnp.float32)
    kernel_terms = []
    for tap_row in range(3):
        for tap_col in range(3):
            shifted = grad_padded[
                :, :, 2 - tap_row : 2 - tap_row + height, 2 - tap_col : 2 - tap_col + width
            ]
            input_grad = input_grad + jnp.einsum(
                "oc,bohw->bchw",
                kernel[tap_row, tap_col],
                shifted,
                preferred_element_type=jnp.float32,
            )
            window = padded[:, :, tap_row : tap_row + height, tap_col : tap_col + width]
            kernel_terms.append(
                jnp.einsum("bohw,bchw->oc", pre_grad, window, preferred_element_type=jnp.float32)
            )
    factor = total ** (-0.5)
    local_kernel = jnp.stack(kernel_terms).reshape(3, 3, channels, channels) * factor
    spatial = lax.psum(local_kernel, ("row", "col"))
    weight_grad = lax.psum_scatter(spatial, "dp", scatter_dimension=2, tiled=True)
    return (input_grad.astype(jnp.bfloat16), weight_grad, sum_norm / total, sum_cot / total)


def solution(mesh):
    return jax.shard_map(
        per_device,
        mesh=mesh,
        in_specs=(P("dp", None, "row", "col"), P(), P(), P("dp", None, "row", "col")),
        out_specs=(P("dp", None, "row", "col"), P(None, None, "dp", None), P(), P()),
        check_vma=False,
    )
```

profile of v0, /device:TPU:0, one launch (start us, length us, event | category | flops | bytes accessed | tf_op | source)
XLA Modules:
  0.0 162.4 jit_solution(4085869104326707929)
XLA Ops:
  7.2 1.9 %copy.26 = bf16[1,64,32,256]{3,1,2,0:T(8,128)(2,1)S(1)} copy(bf16[1,64,32,256]{3,2,1,0:T(8,128)(2,1)} %param.4) | data formatting | bytes 2097152 | tf_op args[0]
  9.2 5.0 %collective-permute-start = (bf16[1,64,1,256]{3,1,2,0:T(8,128)(2,1)S(1)}, bf16[1,64,1,256]{3,1,2,0:T(8,128)(2,1)S(1)}, u32[]{:S(2)}, u32[]{:S(2)}) collective-permute-start(bf16[1,64,1,256]{3,1,2,0:T(8,128)(2,1)S(1)} %get-tuple-element.29), channel_id=1, source_target_pairs={{0,2},{2,4},{4,6},{1,3},{3,5},{5,7},{8,10},{10,12},{12,14},{9,11},... | collective-permute-start | bytes 98312 | tf_op jit(solution)/shard_map/ppermute | solution.py:14
  14.1 1.3 collective-permute-start.1
  15.4 2.2 %fusion.55 = f32[32,256,64]{1,2,0:T(8,128)} fusion(bf16[64,32,256]{2,1,0:T(8,128)(2,1)S(1)} %bitcast.222, bf16[3,3,64,64]{3,2,1,0:T(8,128)(2,1)S(1)} %copy-done.18), kind=kOutput, calls=%fused_computation.92 | convolution fusion | flops 67108864 | bytes 3162112 | tf_op jit(solution)/shard_map/oc,bchw->bohw/dot_general | solution.py:30
  17.7 0.6 constant_dynamic-update-slice_fusion.1
  18.3 1.7 %collective-permute-done.1 = bf16[1,64,1,256]{3,1,2,0:T(8,128)(2,1)S(1)} collective-permute-done((bf16[1,64,1,256]{3,1,2,0:T(8,128)(2,1)S(1)}, bf16[1,64,1,256]{3,1,2,0:T(8,128)(2,1)S(1)}, u32[]{:S(2)}, u32[]{:S(2)}) %collective-permute-start.1) | collective-permute-done | bytes 32800 | tf_op jit(solution)/shard_map/ppermute | solution.py:15
  20.6 1.3 collective-permute-start.3
  22.2 3.0 %collective-permute-start.2 = (bf16[1,64,34,1]{1,2,3,0:T(8,128)(2,1)S(1)}, bf16[1,64,34,1]{1,2,3,0:T(8,128)(2,1)S(1)}, u32[]{:S(2)}, u32[]{:S(2)}) collective-permute-start(bf16[1,64,34,1]{1,2,3,0:T(8,128)(2,1)S(1)} %copy.29), channel_id=1, source_target_pairs={{0,1},{2,3},{4,5},{6,7},{8,9},{10,11},{12,13},{14,15},{16,17},{18,... | collective-permute-start | bytes 13064 | tf_op jit(solution)/shard_map/ppermute | solution.py:14
  25.2 1.8 %fusion.58 = f32[32,256,64]{1,2,0:T(8,128)} fusion(bf16[1,64,32,256]{3,1,2,0:T(8,128)(2,1)S(1)} %copy.26, bf16[1,64,1,256]{3,1,2,0:T(8,128)(2,1)S(1)} %collective-permute-done, bf16[3,3,64,64]{3,2,1,0:T(8,128)(2,1)S(1)} %copy-done.18), kind=kOutput, calls=%fused_computation.94 | convolution fusion | flops 69206016 | bytes 3194880 | tf_op jit(solution)/shard_map/oc,bchw->bohw/dot_general | solution.py:30
  27.0 1.7 %fusion.61 = f32[32,256,64]{1,2,0:T(8,128)} fusion(bf16[1,64,1,256]{3,1,2,0:T(8,128)(2,1)S(1)} %collective-permute-done.1, bf16[1,64,32,256]{3,1,2,0:T(8,128)(2,1)S(1)} %copy.26, bf16[3,3,64,64]{3,2,1,0:T(8,128)(2,1)S(1)} %copy-done.18), kind=kOutput, calls=%fused_computation.95 | convolution fusion | flops 69206016 | bytes 3194880 | tf_op jit(solution)/shard_map/oc,bchw->bohw/dot_general | solution.py:30
  29.1 2.1 %fusion.78 = f32[32,256,64]{1,2,0:T(8,128)} fusion(bf16[3,3,64,64]{3,2,1,0:T(8,128)(2,1)S(1)} %copy-done.18, bf16[1,64,34,256]{3,1,2,0:T(8,128)(2,1)S(1)} %constant_dynamic-update-slice_fusion, bf16[1,64,34,1]{3,1,2,0:T(8,128)(2,1)S(1)} %copy.33), kind=kOutput, calls=%fused_computation.109 | convolution fusion | flops 69206016 | bytes 3784704 | tf_op jit(solution)/shard_map/oc,bchw->bohw/dot_general | solution.py:30
  31.1 2.1 %fusion.86 = f32[32,256,64]{1,2,0:T(8,128)} fusion(bf16[3,3,64,64]{3,2,1,0:T(8,128)(2,1)S(1)} %copy-done.18, bf16[1,64,34,256]{3,1,2,0:T(8,128)(2,1)S(1)} %constant_dynamic-update-slice_fusion, bf16[1,64,34,1]{3,1,2,0:T(8,128)(2,1)S(1)} %copy.33), kind=kOutput, calls=%fused_computation.117 | convolution fusion | flops 69206016 | bytes 3784704 | tf_op jit(solution)/shard_map/oc,bchw->bohw/dot_general | solution.py:30
  33.6 0.6 fusion.83
  34.8 0.6 fusion.64
  35.4 0.6 copy-done.17
  36.0 0.7 copy-done.14
  36.8 0.6 copy-done.15
  37.5 0.7 copy-done.11
  38.3 3.8 %fusion.3 = (f32[64]{0:T(128)S(1)}, f32[64]{0:T(128)S(1)}, f32[64]{0:T(128)S(1)}, f32[32,256,64]{1,2,0:T(8,128)S(1)}) fusion(bf16[1,64,32,256]{3,2,1,0:T(8,128)(2,1)} %param.7, bf16[1,64,34,1]{3,1,2,0:T(8,128)(2,1)S(1)} %copy-done.2, bf16[1,64,34,256]{3,1,2,0:T(8,128)(2,1)S(1)} %constant_dynamic-update-slice_fusion, ...), kind=kOutput, calls=%fused_computation.6 | convolution fusion | flops 76545856 | bytes 21611264 | tf_op jit(solution)/shard_map/oc,bchw->bohw/dot_general | solution.py:30
  42.3 40.6 %all-reduce = (f32[64]{0:T(128)S(1)}, f32[64]{0:T(128)S(1)}, f32[64]{0:T(128)S(1)}, f32[64]{0:T(128)S(1)}) all-reduce(f32[64]{0:T(128)S(1)} %get-tuple-element.13, f32[64]{0:T(128)S(1)} %reduce_sum.37, f32[64]{0:T(128)S(1)} %get-tuple-element.12, f32[64]{0:T(128)S(1)} %get-tuple-element.14), channel_id=1, replica_groups=mesh['dp'=4,'row'=4,'col'=2] {'dp','row','col'}, use_global_device_ids=true, to_apply=%region_1.0 | all-reduce | flops 256 | bytes 2048 | tf_op jit(solution)/shard_map/psum | solution.py:41
  83.0 2.8 %fusion.2 = bf16[1,64,32,256]{3,1,2,0:T(8,128)(2,1)S(1)} fusion(f32[32,256,64]{1,2,0:T(8,128)} %copy-done, f32[64]{0:T(128)S(1)} %get-tuple-element.32, f32[64]{0:T(128)S(1)} %get-tuple-element.20, f32[64]{0:T(128)S(1)} %get-tuple-element.33, f32[64]{0:T(128)S(1)} %get-tuple-element.31, f32[64]{0:T(128)S(1)} %get-tuple-element.19, ...), kind=kLoop, calls=%fused_computation.5 | loop fusion | flops 4194304 | bytes 4195584 | tf_op jit(solution)/shard_map/convert_element_type | solution.py:51
  85.8 0.6 fusion.15
  86.4 1.8 %fusion.52 = f32[32,256,64]{1,2,0:T(8,128)} fusion(bf16[1,64,32,256]{3,1,2,0:T(8,128)(2,1)S(1)} %fusion.2, bf16[3,3,64,64]{3,2,1,0:T(8,128)(2,1)S(1)} %copy-done.18), kind=kOutput, calls=%fused_computation.89 | convolution fusion | flops 67108864 | bytes 3162112 | tf_op jit(solution)/shard_map/oc,bohw->bchw/dot_general | solution.py:60
  88.7 0.6 copy-done.3
  89.3 0.7 fusion.13
  90.0 0.6 fusion.12
  90.6 0.6 copy-done.9
  91.2 1.3 fusion.11
  92.6 0.7 fusion.10
  93.3 0.6 fusion.9
  94.3 0.7 fusion.7
  95.0 1.3 collective-permute-start.5
  96.3 4.5 %collective-permute-start.4 = (bf16[1,64,1,256]{3,1,2,0:T(8,128)(2,1)S(1)}, bf16[1,64,1,256]{3,1,2,0:T(8,128)(2,1)S(1)}, u32[]{:S(2)}, u32[]{:S(2)}) collective-permute-start(bf16[1,64,1,256]{3,1,2,0:T(8,128)(2,1)S(1)} %get-tuple-element.28), channel_id=1, source_target_pairs={{0,2},{2,4},{4,6},{1,3},{3,5},{5,7},{8,10},{10,12},{12,14},{9,11},... | collective-permute-start | bytes 98312 | tf_op jit(solution)/shard_map/ppermute | solution.py:14
  100.9 0.8 broadcast_multiply_fusion
  101.6 0.8 collective-permute-done.4
  103.2 1.3 collective-permute-start.6
  104.8 3.2 %collective-permute-start.7 = (bf16[1,64,34,1]{1,2,3,0:T(8,128)(2,1)S(1)}, bf16[1,64,34,1]{1,2,3,0:T(8,128)(2,1)S(1)}, u32[]{:S(2)}, u32[]{:S(2)}) collective-permute-start(bf16[1,64,34,1]{1,2,3,0:T(8,128)(2,1)S(1)} %copy.41), channel_id=1, source_target_pairs={{0,1},{2,3},{4,5},{6,7},{8,9},{10,11},{12,13},{14,15},{16,17},{18,... | collective-permute-start | bytes 13064 | tf_op jit(solution)/shard_map/ppermute | solution.py:14
  108.1 1.8 %fusion.35 = f32[32,256,64]{1,2,0:T(8,128)} fusion(bf16[1,64,1,256]{3,1,2,0:T(8,128)(2,1)S(1)} %collective-permute-done.5, bf16[1,64,32,256]{3,1,2,0:T(8,128)(2,1)S(1)} %fusion.2, bf16[3,3,64,64]{3,2,1,0:T(8,128)(2,1)S(1)} %copy-done.18), kind=kOutput, calls=%fused_computation.68 | convolution fusion | flops 67633152 | bytes 3194880 | tf_op jit(solution)/shard_map/oc,bohw->bchw/dot_general | solution.py:60
  109.9 1.8 %fusion.27 = f32[32,256,64]{1,2,0:T(8,128)} fusion(bf16[1,64,32,256]{3,1,2,0:T(8,128)(2,1)S(1)} %fusion.2, bf16[1,64,1,256]{3,1,2,0:T(8,128)(2,1)S(1)} %collective-permute-done.4, bf16[3,3,64,64]{3,2,1,0:T(8,128)(2,1)S(1)} %copy-done.18), kind=kOutput, calls=%fused_computation.56 | convolution fusion | flops 67633152 | bytes 3194880 | tf_op jit(solution)/shard_map/oc,bohw->bchw/dot_general | solution.py:60
  112.5 1.4 maximum_maximum_fusion
  114.4 0.6 fusion.32
  116.0 0.6 fusion.38
  117.1 0.6 copy-done.13
  117.7 0.8 copy-done.10
  118.5 1.6 fusion.24
  120.1 1.6 copy.51
  121.6 3.8 %reduce-scatter.2.cloned.1.call-done = f32[3,3,16,64]{3,2,1,0:T(8,128)} async-done(((f32[3,3,64,64]{3,2,1,0:T(8,128)}), f32[3,3,16,64]{3,2,1,0:T(8,128)}) %reduce-scatter.2.cloned.1.call-update) | async-done | bytes 36880 | tf_op jit(solution)/shard_map/reduce_scatter | solution.py:73
  125.5 30.0 %psum.40 = f32[3,3,16,64]{3,2,1,0:T(8,128)} all-reduce(f32[3,3,16,64]{3,2,1,0:T(8,128)} %reduce-scatter.2.cloned.1.call-done), channel_id=1, replica_groups=mesh['dp'=4,'row'=4,'col'=2] {'row','col'}, use_global_device_ids=true, to_apply=%region_8.0 | all-reduce | flops 9216 | bytes 73728 | tf_op jit(solution)/shard_map/psum | solution.py:72
  (68 shorter events, 7.5 us)
Async XLA Ops:
  7.2 8.3 %copy-start.8 = (bf16[1,64,32,256]{3,2,1,0:T(8,128)(2,1)S(1)}, bf16[1,64,32,256]{3,2,1,0:T(8,128)(2,1)}, u32[]{:S(2)}) copy-start(bf16[1,64,32,256]{3,2,1,0:T(8,128)(2,1)} %param.4) | copy-start | bytes 3145732
  7.2 8.3 %copy-start.18 = (bf16[3,3,64,64]{3,2,1,0:T(8,128)(2,1)S(1)}, bf16[3,3,64,64]{3,2,1,0:T(8,128)(2,1)}, u32[]{:S(2)}) copy-start(bf16[3,3,64,64]{3,2,1,0:T(8,128)(2,1)} %param.5) | copy-start | bytes 221188
  7.2 118.3 %reduce-scatter.2.cloned.1.call-start = ((), (), s32[]{:S(2)}) async-start(), calls=%async_computation.1 | async-start | bytes 368640 | tf_op jit(solution)/shard_map/reduce_scatter | solution.py:73
  9.1 17.8 %copy-start.6 = (bf16[1,64,32,256]{3,1,2,0:T(8,128)(2,1)}, bf16[1,64,32,256]{3,1,2,0:T(8,128)(2,1)S(1)}, u32[]{:S(2)}) copy-start(bf16[1,64,32,256]{3,1,2,0:T(8,128)(2,1)S(1)} %copy.26) | copy-start | bytes 3145732
  9.2 8.5 %collective-permute-start = (bf16[1,64,1,256]{3,1,2,0:T(8,128)(2,1)S(1)}, bf16[1,64,1,256]{3,1,2,0:T(8,128)(2,1)S(1)}, u32[]{:S(2)}, u32[]{:S(2)}) collective-permute-start(bf16[1,64,1,256]{3,1,2,0:T(8,128)(2,1)S(1)} %get-tuple-element.29), channel_id=1, source_target_pairs={{0,2},{2,4},{4,6},{1,3},{3,5},{5,7},{8,10},{10,12},{12,14},{9,11},... | collective-permute-start | bytes 98312 | tf_op jit(solution)/shard_map/ppermute | solution.py:14
  14.1 5.8 %collective-permute-start.1 = (bf16[1,64,1,256]{3,1,2,0:T(8,128)(2,1)S(1)}, bf16[1,64,1,256]{3,1,2,0:T(8,128)(2,1)S(1)}, u32[]{:S(2)}, u32[]{:S(2)}) collective-permute-start(bf16[1,64,1,256]{3,1,2,0:T(8,128)(2,1)S(1)} %get-tuple-element.30), channel_id=1, source_target_pairs={{2,0},{4,2},{6,4},{3,1},{5,3},{7,5},{10,8},{12,10},{14,12},{11,9},... | collective-permute-start | bytes 98312 | tf_op jit(solution)/shard_map/ppermute | solution.py:15
  20.6 8.1 %collective-permute-start.3 = (bf16[1,64,34,1]{1,2,3,0:T(8,128)(2,1)S(1)}, bf16[1,64,34,1]{1,2,3,0:T(8,128)(2,1)S(1)}, u32[]{:S(2)}, u32[]{:S(2)}) collective-permute-start(bf16[1,64,34,1]{1,2,3,0:T(8,128)(2,1)S(1)} %copy.32), channel_id=1, source_target_pairs={{1,0},{3,2},{5,4},{7,6},{9,8},{11,10},{13,12},{15,14},{17,16},{19,... | collective-permute-start | bytes 13064 | tf_op jit(solution)/shard_map/ppermute | solution.py:15
  22.2 11.0 %collective-permute-start.2 = (bf16[1,64,34,1]{1,2,3,0:T(8,128)(2,1)S(1)}, bf16[1,64,34,1]{1,2,3,0:T(8,128)(2,1)S(1)}, u32[]{:S(2)}, u32[]{:S(2)}) collective-permute-start(bf16[1,64,34,1]{1,2,3,0:T(8,128)(2,1)S(1)} %copy.29), channel_id=1, source_target_pairs={{0,1},{2,3},{4,5},{6,7},{8,9},{10,11},{12,13},{14,15},{16,17},{18,... | collective-permute-start | bytes 13064 | tf_op jit(solution)/shard_map/ppermute | solution.py:14
  29.1 4.2 %copy-start.1 = (bf16[1,64,34,1]{3,1,2,0:T(8,128)(2,1)}, bf16[1,64,34,1]{3,1,2,0:T(8,128)(2,1)S(1)}, u32[]{:S(2)}) copy-start(bf16[1,64,34,1]{3,1,2,0:T(8,128)(2,1)S(1)} %copy.33) | copy-start | bytes 13060
  33.6 1.2 copy-start.4
  33.6 1.8 %copy-start.16 = (f32[32,256,64]{1,2,0:T(8,128)S(1)}, f32[32,256,64]{1,2,0:T(8,128)}, u32[]{:S(2)}) copy-start(f32[32,256,64]{1,2,0:T(8,128)} %fusion.78) | copy-start | bytes 6291460
  33.6 2.4 %copy-start.17 = (f32[32,256,64]{1,2,0:T(8,128)S(1)}, f32[32,256,64]{1,2,0:T(8,128)}, u32[]{:S(2)}) copy-start(f32[32,256,64]{1,2,0:T(8,128)} %fusion.86) | copy-start | bytes 6291460
  34.2 2.6 %copy-start.14 = (f32[32,256,64]{1,2,0:T(8,128)S(1)}, f32[32,256,64]{1,2,0:T(8,128)}, u32[]{:S(2)}) copy-start(f32[32,256,64]{1,2,0:T(8,128)} %fusion.58) | copy-start | bytes 6291460
  34.2 3.2 %copy-start.15 = (f32[32,256,64]{1,2,0:T(8,128)S(1)}, f32[32,256,64]{1,2,0:T(8,128)}, u32[]{:S(2)}) copy-start(f32[32,256,64]{1,2,0:T(8,128)} %fusion.61) | copy-start | bytes 6291460
  34.8 2.7 %copy-start.2 = (bf16[1,64,34,1]{3,1,2,0:T(8,128)(2,1)S(1)}, bf16[1,64,34,1]{3,1,2,0:T(8,128)(2,1)}, u32[]{:S(2)}) copy-start(bf16[1,64,34,1]{3,1,2,0:T(8,128)(2,1)} %copy-done.1) | copy-start | bytes 13060
  34.8 3.5 %copy-start.11 = (f32[32,256,64]{1,2,0:T(8,128)S(1)}, f32[32,256,64]{1,2,0:T(8,128)}, u32[]{:S(2)}) copy-start(f32[32,256,64]{1,2,0:T(8,128)} %fusion.55) | copy-start | bytes 6291460
  42.1 40.9 %copy-start = (f32[32,256,64]{1,2,0:T(8,128)}, f32[32,256,64]{1,2,0:T(8,128)S(1)}, u32[]{:S(2)}) copy-start(f32[32,256,64]{1,2,0:T(8,128)S(1)} %get-tuple-element.34) | copy-start | bytes 6291460
  42.1 40.9 %copy-start.21 = (f32[64]{0:T(128)S(1)}, f32[64]{0:T(128)}, u32[]{:S(2)}) copy-start(f32[64]{0:T(128)} %param.6) | copy-start | bytes 772
  83.0 2.8 %copy-start.19 = (f32[64]{0:T(128)}, f32[64]{0:T(128)S(1)}, u32[]{:S(2)}) copy-start(f32[64]{0:T(128)S(1)} %get-tuple-element.31) | copy-start | bytes 772
  83.0 2.8 %copy-start.20 = (f32[64]{0:T(128)}, f32[64]{0:T(128)S(1)}, u32[]{:S(2)}) copy-start(f32[64]{0:T(128)S(1)} %get-tuple-element.32) | copy-start | bytes 772
  83.0 2.8 %copy-start.5 = (bf16[1,64,34,1]{3,1,2,0:T(8,128)(2,1)S(1)}, bf16[1,64,34,1]{3,1,2,0:T(8,128)(2,1)}, u32[]{:S(2)}) copy-start(bf16[1,64,34,1]{3,1,2,0:T(8,128)(2,1)} %copy-done.4) | copy-start | bytes 13060
  86.4 1.8 %copy-start.7 = (bf16[1,64,32,256]{3,1,2,0:T(8,128)(2,1)S(1)}, bf16[1,64,32,256]{3,1,2,0:T(8,128)(2,1)}, u32[]{:S(2)}) copy-start(bf16[1,64,32,256]{3,1,2,0:T(8,128)(2,1)} %copy-done.6) | copy-start | bytes 3145732
  88.3 1.1 copy-start.3
  90.0 1.2 copy-start.9
  95.0 6.6 %collective-permute-start.5 = (bf16[1,64,1,256]{3,1,2,0:T(8,128)(2,1)S(1)}, bf16[1,64,1,256]{3,1,2,0:T(8,128)(2,1)S(1)}, u32[]{:S(2)}, u32[]{:S(2)}) collective-permute-start(bf16[1,64,1,256]{3,1,2,0:T(8,128)(2,1)S(1)} %get-tuple-element.27), channel_id=1, source_target_pairs={{2,0},{4,2},{6,4},{3,1},{5,3},{7,5},{10,8},{12,10},{14,12},{11,9},... | collective-permute-start | bytes 98312 | tf_op jit(solution)/shard_map/ppermute | solution.py:15
  96.3 6.1 %collective-permute-start.4 = (bf16[1,64,1,256]{3,1,2,0:T(8,128)(2,1)S(1)}, bf16[1,64,1,256]{3,1,2,0:T(8,128)(2,1)S(1)}, u32[]{:S(2)}, u32[]{:S(2)}) collective-permute-start(bf16[1,64,1,256]{3,1,2,0:T(8,128)(2,1)S(1)} %get-tuple-element.28), channel_id=1, source_target_pairs={{0,2},{2,4},{4,6},{1,3},{3,5},{5,7},{8,10},{10,12},{12,14},{9,11},... | collective-permute-start | bytes 98312 | tf_op jit(solution)/shard_map/ppermute | solution.py:14
  103.2 8.5 %collective-permute-start.6 = (bf16[1,64,34,1]{1,2,3,0:T(8,128)(2,1)S(1)}, bf16[1,64,34,1]{1,2,3,0:T(8,128)(2,1)S(1)}, u32[]{:S(2)}, u32[]{:S(2)}) collective-permute-start(bf16[1,64,34,1]{1,2,3,0:T(8,128)(2,1)S(1)} %copy.37), channel_id=1, source_target_pairs={{1,0},{3,2},{5,4},{7,6},{9,8},{11,10},{13,12},{15,14},{17,16},{19,... | collective-permute-start | bytes 13064 | tf_op jit(solution)/shard_map/ppermute | solution.py:15
  104.8 7.3 %collective-permute-start.7 = (bf16[1,64,34,1]{1,2,3,0:T(8,128)(2,1)S(1)}, bf16[1,64,34,1]{1,2,3,0:T(8,128)(2,1)S(1)}, u32[]{:S(2)}, u32[]{:S(2)}) collective-permute-start(bf16[1,64,34,1]{1,2,3,0:T(8,128)(2,1)S(1)} %copy.41), channel_id=1, source_target_pairs={{0,1},{2,3},{4,5},{6,7},{8,9},{10,11},{12,13},{14,15},{16,17},{18,... | collective-permute-start | bytes 13064 | tf_op jit(solution)/shard_map/ppermute | solution.py:14
  115.5 1.6 copy-start.12
  115.5 2.2 %copy-start.13 = (f32[32,256,64]{1,2,0:T(8,128)S(1)}, f32[32,256,64]{1,2,0:T(8,128)}, u32[]{:S(2)}) copy-start(f32[32,256,64]{1,2,0:T(8,128)} %fusion.27) | copy-start | bytes 6291460
  116.0 2.5 %copy-start.10 = (f32[32,256,64]{1,2,0:T(8,128)S(1)}, f32[32,256,64]{1,2,0:T(8,128)}, u32[]{:S(2)}) copy-start(f32[32,256,64]{1,2,0:T(8,128)} %fusion.52) | copy-start | bytes 6291460
Sparse Core Ops, SparseCore 0:
  101.8 23.6 reduce-scatter.1
where the time goes:
time: 163 us; the launch traced here: 162 us
  blocking collectives  70.7 us (43%)
  matrix products  31.1 us (19%)
  starting transfers between devices  21 us (13%)
  between operations  14.6 us (9%)
  local copies, waits for them, and re-layouts  13.5 us (8%)
  waiting for transfers between devices  6.31 us (4%)
  other arithmetic  5.31 us (3%)
    psum x1, blocking collectives, per_device(): lax.psum((local_pre, local_sq, local_cot, local_cross), ('dp', 'row', 'co...  40.6 us
    psum x1, blocking collectives, per_device(): spatial = lax.psum(local_kernel, ('row', 'col'))  30 us
    ppermute x4, starting transfers between devices, with_halo(): before = lax.ppermute(last, axis, up)  15.8 us
    dot_general x9, matrix products, per_device(): jnp.einsum('oc,bchw->bohw', kernel[tap_row, tap_col], window, preferred_e...  15.4 us
    unnamed x48, local copies, waits for them, and re-layouts  10.1 us
    dot_general x9, matrix products, per_device(): jnp.einsum('oc,bohw->bchw', kernel[tap_row, tap_col], shifted, preferred_...  9.7 us
    dot_general x9, matrix products, per_device(): jnp.einsum('bohw,bchw->oc', pre_grad, window, preferred_element_type=jnp....  5.99 us
    ppermute x4, starting transfers between devices, with_halo(): after = lax.ppermute(initial, axis, down)  5.16 us
  transfers between devices with their start and end apart: 9, of which 3 were waited for; matrix products, arithmetic and copies ran while one was open for 15% of the time, Pallas kernels for 0%

commit v1 on v0

--- a/solution.py
+++ b/solution.py
@@ -69,7 +69,9 @@
             )
     factor = total ** (-0.5)
     local_kernel = jnp.stack(kernel_terms).reshape(3, 3, channels, channels) * factor
-    spatial = lax.psum(local_kernel, ("row", "col"))
+    spatial = local_kernel
+    for mesh_axis in ("row", "col"):
+        spatial = lax.psum(spatial, mesh_axis)
     weight_grad = lax.psum_scatter(spatial, "dp", scatter_dimension=2, tiled=True)
     return (input_grad.astype(jnp.bfloat16), weight_grad, sum_norm / total, sum_cot / total)
 

time: 163 us -> 158 us (0.969)
  blocking collectives: 70.7 us -> 65.2 us
    psum x1 -> x2, blocking collectives: 30 us -> 24.6 us  [per_device(): spatial = lax.psum(spatial, mesh_axis)]
  transfers between devices with their start and end apart: 9 -> 9, of which waited for: 3 -> 3; matrix products, arithmetic and copies ran while one was open for 15% -> 16% of each run, Pallas kernels for 0% -> 0%
where the time goes in v1:
time: 158 us; the launch traced here: 157 us
  blocking collectives  65.2 us (41%)
  matrix products  31.1 us (20%)
  starting transfers between devices  21 us (13%)
  between operations  14.6 us (9%)
  local copies, waits for them, and re-layouts  13.5 us (9%)
  waiting for transfers between devices  6.3 us (4%)
  other arithmetic  5.31 us (3%)
    psum x1, blocking collectives, per_device(): lax.psum((local_pre, local_sq, local_cot, local_cross), ('dp', 'row', 'co...  40.6 us
    psum x2, blocking collectives, per_device(): spatial = lax.psum(spatial, mesh_axis)  24.6 us
    ppermute x4, starting transfers between devices, with_halo(): before = lax.ppermute(last, axis, up)  15.8 us
    dot_general x9, matrix products, per_device(): jnp.einsum('oc,bchw->bohw', kernel[tap_row, tap_col], window, preferred_e...  15.4 us
    unnamed x48, local copies, waits for them, and re-layouts  10.1 us
    dot_general x9, matrix products, per_device(): jnp.einsum('oc,bohw->bchw', kernel[tap_row, tap_col], shifted, preferred_...  9.75 us
    dot_general x9, matrix products, per_device(): jnp.einsum('bohw,bchw->oc', pre_grad, window, preferred_element_type=jnp....  5.99 us
    ppermute x4, starting transfers between devices, with_halo(): after = lax.ppermute(initial, axis, down)  5.16 us
  transfers between devices with their start and end apart: 9, of which 3 were waited for; matrix products, arithmetic and copies ran while one was open for 16% of the time, Pallas kernels for 0%

profile of v1, /device:TPU:0, one launch (start us, length us, event | category | flops | bytes accessed | tf_op | source)
XLA Modules:
  0.0 157.0 jit_solution(7941235415792395592)
XLA Ops:
  7.2 1.9 %copy.26 = bf16[1,64,32,256]{3,1,2,0:T(8,128)(2,1)S(1)} copy(bf16[1,64,32,256]{3,2,1,0:T(8,128)(2,1)} %param.4) | data formatting | bytes 2097152 | tf_op args[0]
  9.2 5.0 %collective-permute-start = (bf16[1,64,1,256]{3,1,2,0:T(8,128)(2,1)S(1)}, bf16[1,64,1,256]{3,1,2,0:T(8,128)(2,1)S(1)}, u32[]{:S(2)}, u32[]{:S(2)}) collective-permute-start(bf16[1,64,1,256]{3,1,2,0:T(8,128)(2,1)S(1)} %get-tuple-element.29), channel_id=1, source_target_pairs={{0,2},{2,4},{4,6},{1,3},{3,5},{5,7},{8,10},{10,12},{12,14},{9,11},... | collective-permute-start | bytes 98312 | tf_op jit(solution)/shard_map/ppermute | solution.py:14
  14.1 1.3 collective-permute-start.1
  15.4 2.2 %fusion.55 = f32[32,256,64]{1,2,0:T(8,128)} fusion(bf16[64,32,256]{2,1,0:T(8,128)(2,1)S(1)} %bitcast.222, bf16[3,3,64,64]{3,2,1,0:T(8,128)(2,1)S(1)} %copy-done.18), kind=kOutput, calls=%fused_computation.92 | convolution fusion | flops 67108864 | bytes 3162112 | tf_op jit(solution)/shard_map/oc,bchw->bohw/dot_general | solution.py:30
  17.7 0.6 constant_dynamic-update-slice_fusion.1
  18.3 1.7 %collective-permute-done.1 = bf16[1,64,1,256]{3,1,2,0:T(8,128)(2,1)S(1)} collective-permute-done((bf16[1,64,1,256]{3,1,2,0:T(8,128)(2,1)S(1)}, bf16[1,64,1,256]{3,1,2,0:T(8,128)(2,1)S(1)}, u32[]{:S(2)}, u32[]{:S(2)}) %collective-permute-start.1) | collective-permute-done | bytes 32800 | tf_op jit(solution)/shard_map/ppermute | solution.py:15
  20.6 1.3 collective-permute-start.3
  22.2 3.0 %collective-permute-start.2 = (bf16[1,64,34,1]{1,2,3,0:T(8,128)(2,1)S(1)}, bf16[1,64,34,1]{1,2,3,0:T(8,128)(2,1)S(1)}, u32[]{:S(2)}, u32[]{:S(2)}) collective-permute-start(bf16[1,64,34,1]{1,2,3,0:T(8,128)(2,1)S(1)} %copy.29), channel_id=1, source_target_pairs={{0,1},{2,3},{4,5},{6,7},{8,9},{10,11},{12,13},{14,15},{16,17},{18,... | collective-permute-start | bytes 13064 | tf_op jit(solution)/shard_map/ppermute | solution.py:14
  25.2 1.8 %fusion.58 = f32[32,256,64]{1,2,0:T(8,128)} fusion(bf16[1,64,32,256]{3,1,2,0:T(8,128)(2,1)S(1)} %copy.26, bf16[1,64,1,256]{3,1,2,0:T(8,128)(2,1)S(1)} %collective-permute-done, bf16[3,3,64,64]{3,2,1,0:T(8,128)(2,1)S(1)} %copy-done.18), kind=kOutput, calls=%fused_computation.94 | convolution fusion | flops 69206016 | bytes 3194880 | tf_op jit(solution)/shard_map/oc,bchw->bohw/dot_general | solution.py:30
  27.0 1.7 %fusion.61 = f32[32,256,64]{1,2,0:T(8,128)} fusion(bf16[1,64,1,256]{3,1,2,0:T(8,128)(2,1)S(1)} %collective-permute-done.1, bf16[1,64,32,256]{3,1,2,0:T(8,128)(2,1)S(1)} %copy.26, bf16[3,3,64,64]{3,2,1,0:T(8,128)(2,1)S(1)} %copy-done.18), kind=kOutput, calls=%fused_computation.95 | convolution fusion | flops 69206016 | bytes 3194880 | tf_op jit(solution)/shard_map/oc,bchw->bohw/dot_general | solution.py:30
  29.1 2.0 %fusion.78 = f32[32,256,64]{1,2,0:T(8,128)} fusion(bf16[3,3,64,64]{3,2,1,0:T(8,128)(2,1)S(1)} %copy-done.18, bf16[1,64,34,256]{3,1,2,0:T(8,128)(2,1)S(1)} %constant_dynamic-update-slice_fusion, bf16[1,64,34,1]{3,1,2,0:T(8,128)(2,1)S(1)} %copy.33), kind=kOutput, calls=%fused_computation.109 | convolution fusion | flops 69206016 | bytes 3784704 | tf_op jit(solution)/shard_map/oc,bchw->bohw/dot_general | solution.py:30
  31.1 2.1 %fusion.86 = f32[32,256,64]{1,2,0:T(8,128)} fusion(bf16[3,3,64,64]{3,2,1,0:T(8,128)(2,1)S(1)} %copy-done.18, bf16[1,64,34,256]{3,1,2,0:T(8,128)(2,1)S(1)} %constant_dynamic-update-slice_fusion, bf16[1,64,34,1]{3,1,2,0:T(8,128)(2,1)S(1)} %copy.33), kind=kOutput, calls=%fused_computation.117 | convolution fusion | flops 69206016 | bytes 3784704 | tf_op jit(solution)/shard_map/oc,bchw->bohw/dot_general | solution.py:30
  35.4 0.6 copy-done.17
  36.0 0.7 copy-done.14
  36.8 0.6 copy-done.15
  37.6 0.7 copy-done.11
  38.3 3.8 %fusion.3 = (f32[64]{0:T(128)S(1)}, f32[64]{0:T(128)S(1)}, f32[64]{0:T(128)S(1)}, f32[32,256,64]{1,2,0:T(8,128)S(1)}) fusion(bf16[1,64,32,256]{3,2,1,0:T(8,128)(2,1)} %param.7, bf16[1,64,34,1]{3,1,2,0:T(8,128)(2,1)S(1)} %copy-done.2, bf16[1,64,34,256]{3,1,2,0:T(8,128)(2,1)S(1)} %constant_dynamic-update-slice_fusion, ...), kind=kOutput, calls=%fused_computation.6 | convolution fusion | flops 76545856 | bytes 21611264 | tf_op jit(solution)/shard_map/oc,bchw->bohw/dot_general | solution.py:30
  42.4 40.6 %all-reduce = (f32[64]{0:T(128)S(1)}, f32[64]{0:T(128)S(1)}, f32[64]{0:T(128)S(1)}, f32[64]{0:T(128)S(1)}) all-reduce(f32[64]{0:T(128)S(1)} %get-tuple-element.13, f32[64]{0:T(128)S(1)} %reduce_sum.37, f32[64]{0:T(128)S(1)} %get-tuple-element.12, f32[64]{0:T(128)S(1)} %get-tuple-element.14), channel_id=1, replica_groups=mesh['dp'=4,'row'=4,'col'=2] {'dp','row','col'}, use_global_device_ids=true, to_apply=%region_1.0 | all-reduce | flops 256 | bytes 2048 | tf_op jit(solution)/shard_map/psum | solution.py:41
  83.1 2.8 %fusion.2 = bf16[1,64,32,256]{3,1,2,0:T(8,128)(2,1)S(1)} fusion(f32[32,256,64]{1,2,0:T(8,128)} %copy-done, f32[64]{0:T(128)S(1)} %get-tuple-element.32, f32[64]{0:T(128)S(1)} %get-tuple-element.20, f32[64]{0:T(128)S(1)} %get-tuple-element.33, f32[64]{0:T(128)S(1)} %get-tuple-element.31, f32[64]{0:T(128)S(1)} %get-tuple-element.19, ...), kind=kLoop, calls=%fused_computation.5 | loop fusion | flops 4194304 | bytes 4195584 | tf_op jit(solution)/shard_map/convert_element_type | solution.py:51
  85.8 0.6 fusion.15
  86.5 1.8 %fusion.52 = f32[32,256,64]{1,2,0:T(8,128)} fusion(bf16[1,64,32,256]{3,1,2,0:T(8,128)(2,1)S(1)} %fusion.2, bf16[3,3,64,64]{3,2,1,0:T(8,128)(2,1)S(1)} %copy-done.18), kind=kOutput, calls=%fused_computation.89 | convolution fusion | flops 67108864 | bytes 3162112 | tf_op jit(solution)/shard_map/oc,bohw->bchw/dot_general | solution.py:60
  88.7 0.6 copy-done.3
  89.3 0.7 fusion.13
  90.0 0.6 fusion.12
  90.6 0.6 copy-done.9
  91.3 1.3 fusion.11
  92.6 0.7 fusion.10
  93.3 0.6 fusion.9
  94.3 0.7 fusion.7
  95.0 1.3 collective-permute-start.5
  96.3 4.5 %collective-permute-start.4 = (bf16[1,64,1,256]{3,1,2,0:T(8,128)(2,1)S(1)}, bf16[1,64,1,256]{3,1,2,0:T(8,128)(2,1)S(1)}, u32[]{:S(2)}, u32[]{:S(2)}) collective-permute-start(bf16[1,64,1,256]{3,1,2,0:T(8,128)(2,1)S(1)} %get-tuple-element.28), channel_id=1, source_target_pairs={{0,2},{2,4},{4,6},{1,3},{3,5},{5,7},{8,10},{10,12},{12,14},{9,11},... | collective-permute-start | bytes 98312 | tf_op jit(solution)/shard_map/ppermute | solution.py:14
  100.9 0.8 broadcast_multiply_fusion
  101.7 0.8 collective-permute-done.4
  103.2 1.3 collective-permute-start.6
  104.8 3.2 %collective-permute-start.7 = (bf16[1,64,34,1]{1,2,3,0:T(8,128)(2,1)S(1)}, bf16[1,64,34,1]{1,2,3,0:T(8,128)(2,1)S(1)}, u32[]{:S(2)}, u32[]{:S(2)}) collective-permute-start(bf16[1,64,34,1]{1,2,3,0:T(8,128)(2,1)S(1)} %copy.41), channel_id=1, source_target_pairs={{0,1},{2,3},{4,5},{6,7},{8,9},{10,11},{12,13},{14,15},{16,17},{18,... | collective-permute-start | bytes 13064 | tf_op jit(solution)/shard_map/ppermute | solution.py:14
  108.1 1.9 %fusion.35 = f32[32,256,64]{1,2,0:T(8,128)} fusion(bf16[1,64,1,256]{3,1,2,0:T(8,128)(2,1)S(1)} %collective-permute-done.5, bf16[1,64,32,256]{3,1,2,0:T(8,128)(2,1)S(1)} %fusion.2, bf16[3,3,64,64]{3,2,1,0:T(8,128)(2,1)S(1)} %copy-done.18), kind=kOutput, calls=%fused_computation.68 | convolution fusion | flops 67633152 | bytes 3194880 | tf_op jit(solution)/shard_map/oc,bohw->bchw/dot_general | solution.py:60
  109.9 1.8 %fusion.27 = f32[32,256,64]{1,2,0:T(8,128)} fusion(bf16[1,64,32,256]{3,1,2,0:T(8,128)(2,1)S(1)} %fusion.2, bf16[1,64,1,256]{3,1,2,0:T(8,128)(2,1)S(1)} %collective-permute-done.4, bf16[3,3,64,64]{3,2,1,0:T(8,128)(2,1)S(1)} %copy-done.18), kind=kOutput, calls=%fused_computation.56 | convolution fusion | flops 67633152 | bytes 3194880 | tf_op jit(solution)/shard_map/oc,bohw->bchw/dot_general | solution.py:60
  112.5 1.4 maximum_maximum_fusion
  113.9 0.6 fusion.30
  114.5 0.6 fusion.32
  116.1 0.6 fusion.38
  117.1 0.6 copy-done.13
  117.8 0.8 copy-done.10
  118.5 1.6 %fusion.24 = bf16[1,64,32,256]{3,1,2,0:T(8,128)(2,1)S(1)} fusion(f32[32,256,64]{1,2,0:T(8,128)S(1)} %copy-done.13, f32[32,256,64]{1,2,0:T(8,128)S(1)} %fusion.30, f32[32,256,64]{1,2,0:T(8,128)S(1)} %fusion.31, f32[32,256,64]{1,2,0:T(8,128)S(1)} %copy-done.10, f32[32,256,64]{1,2,0:T(8,128)S(1)} %fusion.32, f32[32,256,64]{1,2,0:T(8,128)S(1)} %fusion.33, ...), kind=kOutput, calls=%fused_computation.51 | convolution fusion | flops 71827456 | bytes 18890752 | tf_op jit(solution)/shard_map/oc,bohw->bchw/dot_general | solution.py:60
  120.1 1.6 copy.51
  121.7 3.8 %reduce-scatter.2.cloned.1.call-done = f32[3,3,16,64]{3,2,1,0:T(8,128)} async-done(((f32[3,3,64,64]{3,2,1,0:T(8,128)}), f32[3,3,16,64]{3,2,1,0:T(8,128)}) %reduce-scatter.2.cloned.1.call-update) | async-done | bytes 36880 | tf_op jit(solution)/shard_map/reduce_scatter | solution.py:75
  125.5 20.5 %psum.49 = f32[3,3,16,64]{3,2,1,0:T(8,128)S(1)} all-reduce(f32[3,3,16,64]{3,2,1,0:T(8,128)} %reduce-scatter.2.cloned.1.call-done), channel_id=1, replica_groups=mesh['dp'=4,'row'=4,'col'=2] {'row'}, use_global_device_ids=true, to_apply=%region_8.0 | all-reduce | flops 9216 | bytes 73728 | tf_op jit(solution)/shard_map/psum | solution.py:74
  146.0 4.1 %psum.48 = f32[3,3,16,64]{3,2,1,0:T(8,128)} all-reduce(f32[3,3,16,64]{3,2,1,0:T(8,128)S(1)} %psum.49), channel_id=1, replica_groups=mesh['dp'=4,'row'=4,'col'=2] {'col'}, use_global_device_ids=true, to_apply=%region_9.0 | all-reduce | flops 9216 | bytes 73728 | tf_op jit(solution)/shard_map/psum | solution.py:74
  (69 shorter events, 8.1 us)
Async XLA Ops:
  7.2 8.3 %copy-start.8 = (bf16[1,64,32,256]{3,2,1,0:T(8,128)(2,1)S(1)}, bf16[1,64,32,256]{3,2,1,0:T(8,128)(2,1)}, u32[]{:S(2)}) copy-start(bf16[1,64,32,256]{3,2,1,0:T(8,128)(2,1)} %param.4) | copy-start | bytes 3145732
  7.2 8.3 %copy-start.18 = (bf16[3,3,64,64]{3,2,1,0:T(8,128)(2,1)S(1)}, bf16[3,3,64,64]{3,2,1,0:T(8,128)(2,1)}, u32[]{:S(2)}) copy-start(bf16[3,3,64,64]{3,2,1,0:T(8,128)(2,1)} %param.5) | copy-start | bytes 221188
  7.2 118.3 %reduce-scatter.2.cloned.1.call-start = ((), (), s32[]{:S(2)}) async-start(), calls=%async_computation.1 | async-start | bytes 368640 | tf_op jit(solution)/shard_map/reduce_scatter | solution.py:75
  9.1 17.8 %copy-start.6 = (bf16[1,64,32,256]{3,1,2,0:T(8,128)(2,1)}, bf16[1,64,32,256]{3,1,2,0:T(8,128)(2,1)S(1)}, u32[]{:S(2)}) copy-start(bf16[1,64,32,256]{3,1,2,0:T(8,128)(2,1)S(1)} %copy.26) | copy-start | bytes 3145732
  9.2 8.5 %collective-permute-start = (bf16[1,64,1,256]{3,1,2,0:T(8,128)(2,1)S(1)}, bf16[1,64,1,256]{3,1,2,0:T(8,128)(2,1)S(1)}, u32[]{:S(2)}, u32[]{:S(2)}) collective-permute-start(bf16[1,64,1,256]{3,1,2,0:T(8,128)(2,1)S(1)} %get-tuple-element.29), channel_id=1, source_target_pairs={{0,2},{2,4},{4,6},{1,3},{3,5},{5,7},{8,10},{10,12},{12,14},{9,11},... | collective-permute-start | bytes 98312 | tf_op jit(solution)/shard_map/ppermute | solution.py:14
  14.1 5.8 %collective-permute-start.1 = (bf16[1,64,1,256]{3,1,2,0:T(8,128)(2,1)S(1)}, bf16[1,64,1,256]{3,1,2,0:T(8,128)(2,1)S(1)}, u32[]{:S(2)}, u32[]{:S(2)}) collective-permute-start(bf16[1,64,1,256]{3,1,2,0:T(8,128)(2,1)S(1)} %get-tuple-element.30), channel_id=1, source_target_pairs={{2,0},{4,2},{6,4},{3,1},{5,3},{7,5},{10,8},{12,10},{14,12},{11,9},... | collective-permute-start | bytes 98312 | tf_op jit(solution)/shard_map/ppermute | solution.py:15
  20.6 8.2 %collective-permute-start.3 = (bf16[1,64,34,1]{1,2,3,0:T(8,128)(2,1)S(1)}, bf16[1,64,34,1]{1,2,3,0:T(8,128)(2,1)S(1)}, u32[]{:S(2)}, u32[]{:S(2)}) collective-permute-start(bf16[1,64,34,1]{1,2,3,0:T(8,128)(2,1)S(1)} %copy.32), channel_id=1, source_target_pairs={{1,0},{3,2},{5,4},{7,6},{9,8},{11,10},{13,12},{15,14},{17,16},{19,... | collective-permute-start | bytes 13064 | tf_op jit(solution)/shard_map/ppermute | solution.py:15
  22.2 11.1 %collective-permute-start.2 = (bf16[1,64,34,1]{1,2,3,0:T(8,128)(2,1)S(1)}, bf16[1,64,34,1]{1,2,3,0:T(8,128)(2,1)S(1)}, u32[]{:S(2)}, u32[]{:S(2)}) collective-permute-start(bf16[1,64,34,1]{1,2,3,0:T(8,128)(2,1)S(1)} %copy.29), channel_id=1, source_target_pairs={{0,1},{2,3},{4,5},{6,7},{8,9},{10,11},{12,13},{14,15},{16,17},{18,... | collective-permute-start | bytes 13064 | tf_op jit(solution)/shard_map/ppermute | solution.py:14
  29.1 4.1 %copy-start.1 = (bf16[1,64,34,1]{3,1,2,0:T(8,128)(2,1)}, bf16[1,64,34,1]{3,1,2,0:T(8,128)(2,1)S(1)}, u32[]{:S(2)}) copy-start(bf16[1,64,34,1]{3,1,2,0:T(8,128)(2,1)S(1)} %copy.33) | copy-start | bytes 13060
  33.6 1.2 copy-start.4
  33.6 1.8 %copy-start.16 = (f32[32,256,64]{1,2,0:T(8,128)S(1)}, f32[32,256,64]{1,2,0:T(8,128)}, u32[]{:S(2)}) copy-start(f32[32,256,64]{1,2,0:T(8,128)} %fusion.78) | copy-start | bytes 6291460
  33.6 2.4 %copy-start.17 = (f32[32,256,64]{1,2,0:T(8,128)S(1)}, f32[32,256,64]{1,2,0:T(8,128)}, u32[]{:S(2)}) copy-start(f32[32,256,64]{1,2,0:T(8,128)} %fusion.86) | copy-start | bytes 6291460
  34.2 2.6 %copy-start.14 = (f32[32,256,64]{1,2,0:T(8,128)S(1)}, f32[32,256,64]{1,2,0:T(8,128)}, u32[]{:S(2)}) copy-start(f32[32,256,64]{1,2,0:T(8,128)} %fusion.58) | copy-start | bytes 6291460
  34.2 3.2 %copy-start.15 = (f32[32,256,64]{1,2,0:T(8,128)S(1)}, f32[32,256,64]{1,2,0:T(8,128)}, u32[]{:S(2)}) copy-start(f32[32,256,64]{1,2,0:T(8,128)} %fusion.61) | copy-start | bytes 6291460
  34.8 2.7 %copy-start.2 = (bf16[1,64,34,1]{3,1,2,0:T(8,128)(2,1)S(1)}, bf16[1,64,34,1]{3,1,2,0:T(8,128)(2,1)}, u32[]{:S(2)}) copy-start(bf16[1,64,34,1]{3,1,2,0:T(8,128)(2,1)} %copy-done.1) | copy-start | bytes 13060
  34.8 3.5 %copy-start.11 = (f32[32,256,64]{1,2,0:T(8,128)S(1)}, f32[32,256,64]{1,2,0:T(8,128)}, u32[]{:S(2)}) copy-start(f32[32,256,64]{1,2,0:T(8,128)} %fusion.55) | copy-start | bytes 6291460
  42.1 40.9 %copy-start = (f32[32,256,64]{1,2,0:T(8,128)}, f32[32,256,64]{1,2,0:T(8,128)S(1)}, u32[]{:S(2)}) copy-start(f32[32,256,64]{1,2,0:T(8,128)S(1)} %get-tuple-element.34) | copy-start | bytes 6291460
  42.1 40.9 %copy-start.21 = (f32[64]{0:T(128)S(1)}, f32[64]{0:T(128)}, u32[]{:S(2)}) copy-start(f32[64]{0:T(128)} %param.6) | copy-start | bytes 772
  83.0 2.8 %copy-start.19 = (f32[64]{0:T(128)}, f32[64]{0:T(128)S(1)}, u32[]{:S(2)}) copy-start(f32[64]{0:T(128)S(1)} %get-tuple-element.31) | copy-start | bytes 772
  83.0 2.8 %copy-start.20 = (f32[64]{0:T(128)}, f32[64]{0:T(128)S(1)}, u32[]{:S(2)}) copy-start(f32[64]{0:T(128)S(1)} %get-tuple-element.32) | copy-start | bytes 772
  83.0 2.8 %copy-start.5 = (bf16[1,64,34,1]{3,1,2,0:T(8,128)(2,1)S(1)}, bf16[1,64,34,1]{3,1,2,0:T(8,128)(2,1)}, u32[]{:S(2)}) copy-start(bf16[1,64,34,1]{3,1,2,0:T(8,128)(2,1)} %copy-done.4) | copy-start | bytes 13060
  86.4 1.9 %copy-start.7 = (bf16[1,64,32,256]{3,1,2,0:T(8,128)(2,1)S(1)}, bf16[1,64,32,256]{3,1,2,0:T(8,128)(2,1)}, u32[]{:S(2)}) copy-start(bf16[1,64,32,256]{3,1,2,0:T(8,128)(2,1)} %copy-done.6) | copy-start | bytes 3145732
  88.3 1.1 copy-start.3
  90.0 1.2 copy-start.9
  95.0 6.6 %collective-permute-start.5 = (bf16[1,64,1,256]{3,1,2,0:T(8,128)(2,1)S(1)}, bf16[1,64,1,256]{3,1,2,0:T(8,128)(2,1)S(1)}, u32[]{:S(2)}, u32[]{:S(2)}) collective-permute-start(bf16[1,64,1,256]{3,1,2,0:T(8,128)(2,1)S(1)} %get-tuple-element.27), channel_id=1, source_target_pairs={{2,0},{4,2},{6,4},{3,1},{5,3},{7,5},{10,8},{12,10},{14,12},{11,9},... | collective-permute-start | bytes 98312 | tf_op jit(solution)/shard_map/ppermute | solution.py:15
  96.3 6.1 %collective-permute-start.4 = (bf16[1,64,1,256]{3,1,2,0:T(8,128)(2,1)S(1)}, bf16[1,64,1,256]{3,1,2,0:T(8,128)(2,1)S(1)}, u32[]{:S(2)}, u32[]{:S(2)}) collective-permute-start(bf16[1,64,1,256]{3,1,2,0:T(8,128)(2,1)S(1)} %get-tuple-element.28), channel_id=1, source_target_pairs={{0,2},{2,4},{4,6},{1,3},{3,5},{5,7},{8,10},{10,12},{12,14},{9,11},... | collective-permute-start | bytes 98312 | tf_op jit(solution)/shard_map/ppermute | solution.py:14
  103.2 8.5 %collective-permute-start.6 = (bf16[1,64,34,1]{1,2,3,0:T(8,128)(2,1)S(1)}, bf16[1,64,34,1]{1,2,3,0:T(8,128)(2,1)S(1)}, u32[]{:S(2)}, u32[]{:S(2)}) collective-permute-start(bf16[1,64,34,1]{1,2,3,0:T(8,128)(2,1)S(1)} %copy.37), channel_id=1, source_target_pairs={{1,0},{3,2},{5,4},{7,6},{9,8},{11,10},{13,12},{15,14},{17,16},{19,... | collective-permute-start | bytes 13064 | tf_op jit(solution)/shard_map/ppermute | solution.py:15
  104.8 7.3 %collective-permute-start.7 = (bf16[1,64,34,1]{1,2,3,0:T(8,128)(2,1)S(1)}, bf16[1,64,34,1]{1,2,3,0:T(8,128)(2,1)S(1)}, u32[]{:S(2)}, u32[]{:S(2)}) collective-permute-start(bf16[1,64,34,1]{1,2,3,0:T(8,128)(2,1)S(1)} %copy.41), channel_id=1, source_target_pairs={{0,1},{2,3},{4,5},{6,7},{8,9},{10,11},{12,13},{14,15},{16,17},{18,... | collective-permute-start | bytes 13064 | tf_op jit(solution)/shard_map/ppermute | solution.py:14
  115.5 1.6 %copy-start.12 = (f32[32,256,64]{1,2,0:T(8,128)S(1)}, f32[32,256,64]{1,2,0:T(8,128)}, u32[]{:S(2)}) copy-start(f32[32,256,64]{1,2,0:T(8,128)} %fusion.35) | copy-start | bytes 6291460
  115.6 2.2 %copy-start.13 = (f32[32,256,64]{1,2,0:T(8,128)S(1)}, f32[32,256,64]{1,2,0:T(8,128)}, u32[]{:S(2)}) copy-start(f32[32,256,64]{1,2,0:T(8,128)} %fusion.27) | copy-start | bytes 6291460
  116.1 2.5 %copy-start.10 = (f32[32,256,64]{1,2,0:T(8,128)S(1)}, f32[32,256,64]{1,2,0:T(8,128)}, u32[]{:S(2)}) copy-start(f32[32,256,64]{1,2,0:T(8,128)} %fusion.52) | copy-start | bytes 6291460
Sparse Core Ops, SparseCore 0:
  101.8 23.6 reduce-scatter.1
